TPU v7x, 32 devices: a whole 2x2x4 slice. The times are simulated.
32 devices in a mesh: ep: 8 (over z, y), tp: 4 (over x, core).
Axes of the slice: x: 2, y: 2, z: 4, core: 2. Of those that a mesh axis runs over, the one named last changes fastest.
Arguments:
- tokens: bfloat16 [4096, 2048], P(('ep', 'tp')), may hold values from -6 to 6
- norm_gain: float32 [2048], replicated, may hold values from 0.1 to 1.9
- expert_ids: int32 [4096, 6], P(('ep', 'tp')), may hold values from 0 to 15, as said below
- slot_index: int32 [4096, 6], P(('ep', 'tp')), may hold values from 0 to 63, as said below
- dropped: int32 [4096, 6], P(('ep', 'tp')), may hold values from 0 to 1, as said below
- gates: float32 [4096, 6], P(('ep', 'tp')), may hold values from 0.05 to 0.8
- w_gate: bfloat16 [16, 2048, 704], P('ep', None, 'tp'), may hold values from -0.125 to 0.125
- w_up: bfloat16 [16, 2048, 704], P('ep', None, 'tp'), may hold values from -0.125 to 0.125
- w_down: bfloat16 [16, 2048, 704], P('ep', None, 'tp'), may hold values from -0.21875 to 0.21875
- shared_gate: bfloat16 [2048, 1408], P(None, 'tp'), may hold values from -0.125 to 0.125
- shared_up: bfloat16 [2048, 1408], P(None, 'tp'), may hold values from -0.125 to 0.125
- shared_down: bfloat16 [1408, 2048], replicated, may hold values from -0.15625 to 0.15625
Outputs:
- layer_out: bfloat16 [4096, 2048], P(('ep', 'tp'))
Inputs may be any that keep to these rules, and one draw needn't show every extreme that they name: `expert_ids`: each token names 6 different experts; some expert has 64 kept pairs from the tokens of every device. `slot_index`: for a kept pair, its place among the slots of its expert for the tokens of its device (the tokens n with one value of n // 128); the kept pairs of one device and one expert have distinct places; 0 for a dropped pair. `dropped`: 1 for the pairs of a device and an expert beyond the 64 that are kept.
All inputs are finite; a program needn't handle non-finite values.
Results may differ from a plain program's by a relative error of at most 0.0054.
Values may be sent and summed in bfloat16 or wider, within the bound.
A program may use at most 128 MiB of HBM per device.

v0:
```python
import jax
import jax.numpy as jnp
from jax import lax
from jax.sharding import PartitionSpec as P

TOP = 6
EXP_DEV = 2
TOK_DEV = 128
norm_eps = 1e-06


def swiglu(left, right):
    return jax.nn.silu(left) * right


def on_device(
    tokens,
    norm_gain,
    expert_ids,
    slot_index,
    dropped,
    gates,
    w_gate,
    w_up,
    w_down,
    shared_gate,
    shared_up,
    shared_down,
):
    n_expert_groups = lax.axis_size("ep")
    experts = EXP_DEV * n_expert_groups
    capacity = TOK_DEV * TOP * 4 // (experts * 3)
    model_width = tokens.shape[1]
    local_rows = tokens.shape[0]
    values = tokens.astype(jnp.float32)
    scale = lax.rsqrt(jnp.mean(values * values, axis=-1, keepdims=True) + norm_eps)
    normed = (values * scale * norm_gain).astype(jnp.bfloat16)
    destination_position = expert_ids * capacity + slot_index
    kept_pair = dropped == 0
    matrix_breadth = lax.iota(jnp.int32, experts * capacity)
    matches = (destination_position[:, :, None] == matrix_breadth[None, None, :]) & kept_pair[
        :, :, None
    ]
    dispatch_table = jnp.any(matches, axis=1).astype(jnp.bfloat16)
    outgoing = lax.dot_general(
        dispatch_table, normed, (((0,), (0,)), ((), ())), preferred_element_type=jnp.float32
    ).astype(jnp.bfloat16)
    boxes = outgoing.reshape(n_expert_groups, EXP_DEV, capacity, model_width)
    received = lax.all_to_all(boxes, "ep", split_axis=0, concat_axis=0, tiled=True)
    gate_all = lax.all_gather(w_gate, "tp", axis=2, tiled=True)
    up_all = lax.all_gather(w_up, "tp", axis=2, tiled=True)
    down_all = lax.all_gather(w_down, "tp", axis=2, tiled=True)
    gate_act = jnp.einsum("iecd,edf->iecf", received, gate_all, preferred_element_type=jnp.float32)
    up_act = jnp.einsum("iecd,edf->iecf", received, up_all, preferred_element_type=jnp.float32)
    hidden = swiglu(gate_act, up_act).astype(jnp.bfloat16)
    expert_out = jnp.einsum(
        "iecf,edf->iecd", hidden, down_all, preferred_element_type=jnp.float32
    ).astype(jnp.bfloat16)
    returned_output = lax.all_to_all(expert_out, "ep", split_axis=0, concat_axis=0, tiled=True)
    returned_rows = returned_output.reshape(experts * capacity, model_width)
    shard_piece = lax.all_gather(normed, "tp", axis=0, tiled=True)
    gate_act = jnp.dot(shard_piece, shared_gate, preferred_element_type=jnp.float32)
    up_act = jnp.dot(shard_piece, shared_up, preferred_element_type=jnp.float32)
    partial_hidden = swiglu(gate_act, up_act).astype(jnp.bfloat16)
    whole_hidden = lax.all_to_all(partial_hidden, "tp", split_axis=0, concat_axis=1, tiled=True)
    shared_out = jnp.dot(whole_hidden, shared_down, preferred_element_type=jnp.float32)
    safe_target = jnp.where(kept_pair, destination_position, 0)
    picked = jnp.take(returned_rows, safe_target.reshape(-1), axis=0).reshape(
        local_rows, TOP, model_width
    )
    kept_weights = jnp.where(kept_pair, gates, jnp.float32(0.0))
    routed = jnp.sum(picked.astype(jnp.float32) * kept_weights[:, :, None], axis=1)
    return (values + shared_out + routed).astype(jnp.bfloat16)


def solution(mesh):
    placed = (
        P(("ep", "tp"), None),
        P(),
        P(("ep", "tp"), None),
        P(("ep", "tp"), None),
        P(("ep", "tp"), None),
        P(("ep", "tp"), None),
        P("ep", None, "tp"),
        P("ep", None, "tp"),
        P("ep", None, "tp"),
        P(None, "tp"),
        P(None, "tp"),
        P(),
    )
    return jax.shard_map(
        on_device, mesh=mesh, in_specs=placed, out_specs=P(("ep", "tp"), None), check_vma=False
    )
```

profile of v0, /device:TPU:0, one launch (start us, length us, event | category | flops | bytes accessed | tf_op | source)
XLA Modules:
  0.0 298.9 jit_solution(15551164740821854965)
XLA Ops:
  6.6 0.0 all-gather.9.cloned.1.call-start
  6.6 0.7 all-gather.9.cloned.1.call-update
  7.3 0.0 all-gather.11.cloned.1.call-start
  7.3 0.7 all-gather.11.cloned.1.call-update
  8.0 0.0 all-gather.7.cloned.1.call-start
  8.1 0.7 all-gather.7.cloned.1.call-update
  8.8 0.2 fusion.29
  9.0 0.2 fusion.31
  9.3 0.6 fusion.15
  9.9 1.3 convolution_convert_fusion
  11.2 100.4 %all_to_all.29 = bf16[8,2,64,2048]{3,2,1,0:T(8,128)(2,1)} all-to-all(bf16[8,2,64,2048]{3,2,1,0:T(8,128)(2,1)S(1)} %bitcast.62), channel_id=1, replica_groups=mesh['ep'=8,'tp'=4] {'ep'}, dimensions={0} | all-to-all | bytes 8388608 | tf_op jit(solution)/shard_map/all_to_all | solution.py:49
  111.5 9.2 %fusion.2 = f32[2,8,64,704]{3,2,1,0:T(8,128)} fusion(bf16[2,2048,704]{1,2,0:T(8,128)(2,1)} %all-gather.9.cloned.1.call-done, bf16[8,2,64,2048]{3,2,1,0:T(8,128)(2,1)} %all_to_all.29), kind=kOutput, calls=%fused_computation.4 | convolution fusion | flops 2952790016 | bytes 12845056 | tf_op jit(solution)/shard_map/iecd,edf->iecf/dot_general | solution.py:54
  120.7 24.3 %all-gather.7.cloned.1.call-done = bf16[2,2048,704]{1,2,0:T(8,128)(2,1)} async-done(((bf16[2,2048,176]{1,2,0:T(8,128)(2,1)}), bf16[2,2048,704]{1,2,0:T(8,128)(2,1)}) %all-gather.7.cloned.1.call-update) | async-done | bytes 5767184 | tf_op jit(solution)/shard_map/all_gather | solution.py:50
  145.0 13.1 %convert_bitcast_fusion = bf16[8,2,64,2048]{3,2,0,1:T(8,128)(2,1)} fusion(bf16[2,2048,704]{1,2,0:T(8,128)(2,1)} %all-gather.11.cloned.1.call-done, f32[2,8,64,704]{3,2,1,0:T(8,128)} %fusion.2, bf16[2,2048,704]{1,2,0:T(8,128)(2,1)} %all-gather.7.cloned.1.call-done, bf16[8,2,64,2048]{3,2,1,0:T(8,128)(2,1)} %all_to_all.29), kind=kOutput, calls=%fused_computation.8 | convolution fusion | flops 5912002560 | bytes 22806528 | tf_op jit(solution)/shard_map/iecf,edf->iecd/dot_general | solution.py:56
  158.1 4.7 %copy.39 = bf16[8,2,64,2048]{3,2,1,0:T(8,128)(2,1)} copy(bf16[8,2,64,2048]{3,2,0,1:T(8,128)(2,1)} %convert_bitcast_fusion) | data formatting | bytes 8388608 | tf_op jit(solution)/shard_map/convert_element_type | solution.py:58
  162.9 5.6 %all-to-all-start.2 = ((bf16[8,2,64,2048]{3,2,1,0:T(8,128)(2,1)}), bf16[8,2,64,2048]{3,2,1,0:T(8,128)(2,1)}, u32[]{:S(2)}, u32[]{:S(2)}) async-start(bf16[8,2,64,2048]{3,2,1,0:T(8,128)(2,1)} %copy.39), calls=%async_computation.2 | async-start | bytes 8388608 | tf_op jit(solution)/shard_map/all_to_all | solution.py:59
  168.5 0.0 all-gather.5.cloned.1.call-start
  168.6 0.5 all-gather.5.cloned.1.call-update
  169.1 0.1 copy.40
  169.2 0.1 reshape.66
  169.4 0.1 copy.41
  169.5 0.1 copy.36
  169.7 24.0 %all-gather.5.cloned.1.call-done = bf16[512,2048]{1,0:T(8,128)(2,1)} async-done(((bf16[128,2048]{1,0:T(8,128)(2,1)}), bf16[512,2048]{1,0:T(8,128)(2,1)}) %all-gather.5.cloned.1.call-update) | async-done | bytes 2097168 | tf_op jit(solution)/shard_map/all_gather | solution.py:61
  193.7 2.7 fusion.34
  196.4 2.4 fusion.28
  198.8 0.8 copy.55
  199.6 62.6 %all-to-all-done.2 = bf16[8,2,64,2048]{3,2,1,0:T(8,128)(2,1)} async-done(((bf16[8,2,64,2048]{3,2,1,0:T(8,128)(2,1)}), bf16[8,2,64,2048]{3,2,1,0:T(8,128)(2,1)}, u32[]{:S(2)}, u32[]{:S(2)}) %all-to-all-start.2) | async-done | bytes 4194336 | tf_op jit(solution)/shard_map/all_to_all | solution.py:59
  262.2 3.6 %all-to-all-start = ((bf16[4,128,352]{1,2,0:T(8,128)(2,1)}), bf16[4,128,352]{1,2,0:T(8,128)(2,1)S(1)}, u32[]{:S(2)}, u32[]{:S(2)}) async-start(bf16[4,128,352]{1,2,0:T(8,128)(2,1)} %bitcast.61), calls=%async_computation | async-start | bytes 720896 | tf_op jit(solution)/shard_map/all_to_all | solution.py:65
  265.9 9.9 %gather_fusion = bf16[768,2048]{1,0:T(8,128)(2,1)} fusion(bf16[1024,2048]{1,0:T(8,128)(2,1)} %bitcast.12, s32[1024]{0:T(1024)S(1)} %pad_clamp_fusion), kind=kCustom, calls=%fused_computation | custom fusion | bytes 6294528 | tf_op jit(solution)/shard_map/jit(_take)/gather | solution.py:68
  275.7 6.2 %gather.7 = bf16[128,6,2048]{2,1,0:T(8,128)(2,1)} reshape(bf16[768,2048]{1,0:T(8,128)(2,1)} %gather_fusion) | data formatting | bytes 6291456 | tf_op jit(solution)/shard_map/jit(_take)/gather | solution.py:68
  282.0 6.0 %multiply_reduce_fusion = f32[128,2048]{1,0:T(8,128)S(1)} fusion(f32[128,6]{1,0:T(8,128)S(1)} %copy.41, bf16[128,6,2048]{2,1,0:T(8,128)(2,1)} %gather.7, pred[128,6]{1,0:T(8,128)(4,1)S(1)} %copy.36), kind=kLoop, calls=%fused_computation.1 | loop fusion | flops 6029312 | bytes 4198144 | tf_op jit(solution)/shard_map/reduce_sum | solution.py:72
  287.9 4.4 %fusion.17 = bf16[128,2048]{1,0:T(8,128)(2,1)} fusion(f32[128,2048]{1,0:T(8,128)S(1)} %multiply_reduce_fusion, bf16[128,1408]{0,1:T(8,128)(2,1)S(1)} %bitcast.63, bf16[1408,2048]{1,0:T(8,128)(2,1)} %param.23, bf16[128,2048]{1,0:T(8,128)(2,1)S(1)} %copy-done.1), kind=kOutput, calls=%fused_computation.24 | convolution fusion | flops 739246080 | bytes 8224768 | tf_op jit(solution)/shard_map/dot_general | solution.py:66
  (26 shorter events, 0.1 us)
Async XLA Ops:
  6.5 187.1 %copy-start = (bf16[2048,352]{0,1:T(8,128)(2,1)S(1)}, bf16[2048,352]{0,1:T(8,128)(2,1)}, u32[]{:S(2)}) copy-start(bf16[2048,352]{0,1:T(8,128)(2,1)} %param.21) | copy-start | bytes 4325380
  6.5 2.2 copy-start.1
  6.5 2.4 copy-start.3
  6.5 2.7 copy-start.6
  6.5 2.7 copy-start.5
  6.5 2.7 copy-start.7
  6.6 105.0 %all-gather.9.cloned.1.call-start = ((), (), s32[]{:S(2)}) async-start(), calls=%async_computation.5 | async-start | bytes 7208960 | tf_op jit(solution)/shard_map/all_gather | solution.py:51
  7.3 113.4 %all-gather.11.cloned.1.call-start = ((), (), s32[]{:S(2)}) async-start(), calls=%async_computation.6 | async-start | bytes 7208960 | tf_op jit(solution)/shard_map/all_gather | solution.py:52
  8.0 137.0 %all-gather.7.cloned.1.call-start = ((), (), s32[]{:S(2)}) async-start(), calls=%async_computation.4 | async-start | bytes 7208960 | tf_op jit(solution)/shard_map/all_gather | solution.py:50
  9.2 102.4 %copy-start.2 = (bf16[128,2048]{1,0:T(8,128)(2,1)}, bf16[128,2048]{1,0:T(8,128)(2,1)S(1)}, u32[]{:S(2)}) copy-start(bf16[128,2048]{1,0:T(8,128)(2,1)S(1)} %fusion.31) | copy-start | bytes 1572868
  162.9 6.5 %copy-start.4 = (f32[128,6]{0,1:T(8,128)S(1)}, f32[128,6]{0,1:T(8,128)}, u32[]{:S(2)}) copy-start(f32[128,6]{0,1:T(8,128)} %param.17) | copy-start | bytes 9220
  162.9 99.3 %all-to-all-start.2 = ((bf16[8,2,64,2048]{3,2,1,0:T(8,128)(2,1)}), bf16[8,2,64,2048]{3,2,1,0:T(8,128)(2,1)}, u32[]{:S(2)}, u32[]{:S(2)}) async-start(bf16[8,2,64,2048]{3,2,1,0:T(8,128)(2,1)} %copy.39), calls=%async_computation.2 | async-start | bytes 8388608 | tf_op jit(solution)/shard_map/all_to_all | solution.py:59
  168.5 25.1 %all-gather.5.cloned.1.call-start = ((), (), s32[]{:S(2)}) async-start(), calls=%async_computation.3 | async-start | bytes 2621440 | tf_op jit(solution)/shard_map/all_gather | solution.py:61
  193.7 2.7 copy-start.8
  262.2 25.7 %all-to-all-start = ((bf16[4,128,352]{1,2,0:T(8,128)(2,1)}), bf16[4,128,352]{1,2,0:T(8,128)(2,1)S(1)}, u32[]{:S(2)}, u32[]{:S(2)}) async-start(bf16[4,128,352]{1,2,0:T(8,128)(2,1)} %bitcast.61), calls=%async_computation | async-start | bytes 720896 | tf_op jit(solution)/shard_map/all_to_all | solution.py:65
Sparse Core Ops, SparseCore 0:
  8.9 46.0 all-gather.8
  56.6 43.3 all-gather.10
  101.6 43.3 all-gather.6
  170.6 23.0 all-gather.4
where the time goes:
time: 300 us; the launch traced here: 299 us
  waiting for transfers between devices  114 us (38%)
  blocking collectives  100 us (33%)
  matrix products  33.2 us (11%)
  local copies, waits for them, and re-layouts  22.2 us (7%)
  between operations  13.3 us (4%)
  starting transfers between devices  9.44 us (3%)
  other arithmetic  6.97 us (2%)
    all_to_all x1, blocking collectives, on_device(): lax.all_to_all(boxes, 'ep', split_axis=0, concat_axis=0, tiled=True)  100 us
    all_to_all x1, waiting for transfers between devices, on_device(): lax.all_to_all(expert_out, 'ep', split_axis=0, concat_axis=0, tiled=True)  62.6 us
    all_gather x1, waiting for transfers between devices, on_device(): gate_all = lax.all_gather(w_gate, 'tp', axis=2, tiled=True)  24.3 us
    all_gather x1, waiting for transfers between devices, on_device(): shard_piece = lax.all_gather(normed, 'tp', axis=0, tiled=True)  24 us
    gather x2, local copies, waits for them, and re-layouts, on_device(): jnp.take(returned_rows, safe_target.reshape(-1), axis=0)  16.1 us
    dot_general x1, matrix products, on_device(): jnp.einsum('iecf,edf->iecd', hidden, down_all, preferred_element_type=jnp...  13.1 us
    dot_general x1, matrix products, on_device(): jnp.einsum('iecd,edf->iecf', received, up_all, preferred_element_type=jnp...  9.17 us
  transfers between devices with their start and end apart: 6, of which 3 were waited for; matrix products, arithmetic and copies ran while one was open for 13% of the time, Pallas kernels for 0%

commit v1 on v0

--- a/solution.py
+++ b/solution.py
@@ -58,7 +58,12 @@
     ).astype(jnp.bfloat16)
     returned_output = lax.all_to_all(expert_out, "ep", split_axis=0, concat_axis=0, tiled=True)
     returned_rows = returned_output.reshape(experts * capacity, model_width)
-    shard_piece = lax.all_gather(normed, "tp", axis=0, tiled=True)
+    ring = [normed]
+    for hop in range(3):
+        ring.append(lax.ppermute(ring[-1], "tp", [(dev, (dev + 1) % 4) for dev in range(4)]))
+    shard_piece = jnp.roll(
+        jnp.concatenate(ring[::-1], axis=0), (lax.axis_index("tp") + 1) * ring[0].shape[0], axis=0
+    )
     gate_act = jnp.dot(shard_piece, shared_gate, preferred_element_type=jnp.float32)
     up_act = jnp.dot(shard_piece, shared_up, preferred_element_type=jnp.float32)
     partial_hidden = swiglu(gate_act, up_act).astype(jnp.bfloat16)

time: 300 us -> 299 us (level)
  local copies, waits for them, and re-layouts: 22.2 us -> 26.3 us
  waiting for transfers between devices: 114 us -> 110 us
  matrix products: 33.2 us -> 29.9 us
  other arithmetic: 6.97 us -> 10.1 us
    all_gather x1, waiting for transfers between devices: 24.3 us -> 0.01 us  [on_device(): gate_all = lax.all_gather(w_gate, 'tp', axis=2, tiled=True)]
    all_gather x1 -> x0, waiting for transfers between devices: 24 us -> none  [on_device(): shard_piece = lax.all_gather(normed, 'tp', axis=0, tiled=True)]
    all_gather x1, waiting for transfers between devices: 0.01 us -> 23.4 us  [on_device(): down_all = lax.all_gather(w_down, 'tp', axis=2, tiled=True)]
    ppermute x0 -> x3, waiting for transfers between devices: none -> 21.2 us  [on_device(): lax.ppermute(ring[-1], 'tp', [(dev, (dev + 1) % 4) for dev in range(4)])]
  transfers between devices with their start and end apart: 6 -> 8, of which waited for: 3 -> 5; matrix products, arithmetic and copies ran while one was open for 13% -> 15% of each run, Pallas kernels for 0% -> 0%
where the time goes in v1:
time: 299 us
  waiting for transfers between devices  110 us (37%)
  blocking collectives  100 us (33%)
  matrix products  29.9 us (10%)
  local copies, waits for them, and re-layouts  26.3 us (9%)
  between operations  13.3 us (4%)
  other arithmetic  10.1 us (3%)
  starting transfers between devices  9.1 us (3%)
    all_to_all x1, blocking collectives, on_device(): lax.all_to_all(boxes, 'ep', split_axis=0, concat_axis=0, tiled=True)  100 us
    all_to_all x1, waiting for transfers between devices, on_device(): lax.all_to_all(expert_out, 'ep', split_axis=0, concat_axis=0, tiled=True)  62.9 us
    all_gather x1, waiting for transfers between devices, on_device(): down_all = lax.all_gather(w_down, 'tp', axis=2, tiled=True)  23.4 us
    ppermute x3, waiting for transfers between devices, on_device(): lax.ppermute(ring[-1], 'tp', [(dev, (dev + 1) % 4) for dev in range(4)])  21.2 us
    gather x2, local copies, waits for them, and re-layouts, on_device(): jnp.take(returned_rows, safe_target.reshape(-1), axis=0)  16.1 us
    dot_general x1, matrix products, on_device(): jnp.einsum('iecf,edf->iecd', hidden, down_all, preferred_element_type=jnp...  13.1 us
    dot_general x1, matrix products, on_device(): jnp.einsum('iecd,edf->iecf', received, up_all, preferred_element_type=jnp...  8.98 us
  transfers between devices with their start and end apart: 8, of which 5 were waited for; matrix products, arithmetic and copies ran while one was open for 15% of the time, Pallas kernels for 0%

profile of v1, /device:TPU:0, one launch (start us, length us, event | category | flops | bytes accessed | tf_op | source)
XLA Modules:
  0.0 298.7 jit_solution(5645106279037805128)
XLA Ops:
  6.6 0.7 all-gather.6.cloned.1.call-update
  7.3 0.7 all-gather.4.cloned.1.call-update
  8.1 0.7 all-gather.8.cloned.1.call-update
  9.0 0.6 copy-done.6
  9.8 0.6 compare_and_fusion
  10.4 0.6 fusion.15
  11.0 1.3 convolution_convert_fusion
  12.3 100.4 %all_to_all.29 = bf16[8,2,64,2048]{3,2,1,0:T(8,128)(2,1)} all-to-all(bf16[8,2,64,2048]{3,2,1,0:T(8,128)(2,1)S(1)} %bitcast.60), channel_id=1, replica_groups=mesh['ep'=8,'tp'=4] {'ep'}, dimensions={0} | all-to-all | bytes 8388608 | tf_op jit(solution)/shard_map/all_to_all | solution.py:49
  112.7 9.0 %fusion.2 = f32[2,8,64,704]{3,2,1,0:T(8,128)} fusion(bf16[2,2048,704]{1,2,0:T(8,128)(2,1)} %all-gather.6.cloned.1.call-done, bf16[8,2,64,2048]{3,2,1,0:T(8,128)(2,1)} %all_to_all.29), kind=kOutput, calls=%fused_computation.4 | convolution fusion | flops 2952790016 | bytes 12845056 | tf_op jit(solution)/shard_map/iecd,edf->iecf/dot_general | solution.py:54
  121.7 23.4 %all-gather.8.cloned.1.call-done = bf16[2,2048,704]{1,2,0:T(8,128)(2,1)} async-done(((bf16[2,2048,176]{1,2,0:T(8,128)(2,1)}), bf16[2,2048,704]{1,2,0:T(8,128)(2,1)}) %all-gather.8.cloned.1.call-update) | async-done | bytes 5767184 | tf_op jit(solution)/shard_map/all_gather | solution.py:52
  145.0 13.1 %convert_bitcast_fusion = bf16[8,2,64,2048]{3,2,0,1:T(8,128)(2,1)} fusion(bf16[2,2048,704]{1,2,0:T(8,128)(2,1)} %all-gather.8.cloned.1.call-done, f32[2,8,64,704]{3,2,1,0:T(8,128)} %fusion.2, bf16[2,2048,704]{1,2,0:T(8,128)(2,1)} %all-gather.4.cloned.1.call-done, bf16[8,2,64,2048]{3,2,1,0:T(8,128)(2,1)} %all_to_all.29), kind=kOutput, calls=%fused_computation.8 | convolution fusion | flops 5912002560 | bytes 22806528 | tf_op jit(solution)/shard_map/iecf,edf->iecd/dot_general | solution.py:56
  158.2 4.8 %copy.39 = bf16[8,2,64,2048]{3,2,1,0:T(8,128)(2,1)} copy(bf16[8,2,64,2048]{3,2,0,1:T(8,128)(2,1)} %convert_bitcast_fusion) | data formatting | bytes 8388608 | tf_op jit(solution)/shard_map/convert_element_type | solution.py:58
  162.9 5.5 %all-to-all-start.2 = ((bf16[8,2,64,2048]{3,2,1,0:T(8,128)(2,1)}), bf16[8,2,64,2048]{3,2,1,0:T(8,128)(2,1)}, u32[]{:S(2)}, u32[]{:S(2)}) async-start(bf16[8,2,64,2048]{3,2,1,0:T(8,128)(2,1)} %copy.39), calls=%async_computation.2 | async-start | bytes 8388608 | tf_op jit(solution)/shard_map/all_to_all | solution.py:59
  168.4 8.6 %collective-permute-done = bf16[128,2048]{1,0:T(8,128)(2,1)S(1)} collective-permute-done((bf16[128,2048]{1,0:T(8,128)(2,1)S(1)}, bf16[128,2048]{1,0:T(8,128)(2,1)S(1)}, u32[]{:S(2)}, u32[]{:S(2)}) %collective-permute-start) | collective-permute-done | bytes 524320 | tf_op jit(solution)/shard_map/ppermute | solution.py:63
  177.0 8.6 %collective-permute-done.1 = bf16[128,2048]{1,0:T(8,128)(2,1)S(1)} collective-permute-done((bf16[128,2048]{1,0:T(8,128)(2,1)S(1)}, bf16[128,2048]{1,0:T(8,128)(2,1)S(1)}, u32[]{:S(2)}, u32[]{:S(2)}) %collective-permute-start.1) | collective-permute-done | bytes 524320 | tf_op jit(solution)/shard_map/ppermute | solution.py:63
  185.7 0.7 copy.40
  186.4 1.0 reshape.66
  187.4 0.7 broadcast_select_fusion
  188.1 0.7 copy.41
  188.8 1.4 copy.36
  190.2 4.0 %collective-permute-done.2 = bf16[128,2048]{1,0:T(8,128)(2,1)S(1)} collective-permute-done((bf16[128,2048]{1,0:T(8,128)(2,1)S(1)}, bf16[128,2048]{1,0:T(8,128)(2,1)S(1)}, u32[]{:S(2)}, u32[]{:S(2)}) %collective-permute-start.2) | collective-permute-done | bytes 524320 | tf_op jit(solution)/shard_map/ppermute | solution.py:63
  194.4 0.9 constant_dynamic-update-slice_fusion.4
  195.4 1.0 constant_dynamic-update-slice_fusion
  196.4 1.0 fusion.28
  197.4 1.0 fusion.34
  198.4 0.8 copy.55
  199.2 62.9 %all-to-all-done.2 = bf16[8,2,64,2048]{3,2,1,0:T(8,128)(2,1)} async-done(((bf16[8,2,64,2048]{3,2,1,0:T(8,128)(2,1)}), bf16[8,2,64,2048]{3,2,1,0:T(8,128)(2,1)}, u32[]{:S(2)}, u32[]{:S(2)}) %all-to-all-start.2) | async-done | bytes 4194336 | tf_op jit(solution)/shard_map/all_to_all | solution.py:59
  262.1 3.5 %all-to-all-start = ((bf16[4,128,352]{1,2,0:T(8,128)(2,1)}), bf16[4,128,352]{1,2,0:T(8,128)(2,1)S(1)}, u32[]{:S(2)}, u32[]{:S(2)}) async-start(bf16[4,128,352]{1,2,0:T(8,128)(2,1)} %bitcast.59), calls=%async_computation | async-start | bytes 720896 | tf_op jit(solution)/shard_map/all_to_all | solution.py:70
  265.6 9.8 %gather_fusion = bf16[768,2048]{1,0:T(8,128)(2,1)} fusion(bf16[1024,2048]{1,0:T(8,128)(2,1)} %bitcast.12, s32[1024]{0:T(1024)S(1)} %pad_clamp_fusion), kind=kCustom, calls=%fused_computation | custom fusion | bytes 6294528 | tf_op jit(solution)/shard_map/jit(_take)/gather | solution.py:73
  275.4 6.3 %gather.7 = bf16[128,6,2048]{2,1,0:T(8,128)(2,1)} reshape(bf16[768,2048]{1,0:T(8,128)(2,1)} %gather_fusion) | data formatting | bytes 6291456 | tf_op jit(solution)/shard_map/jit(_take)/gather | solution.py:73
  281.7 6.0 %multiply_reduce_fusion = f32[128,2048]{1,0:T(8,128)S(1)} fusion(f32[128,6]{1,0:T(8,128)S(1)} %copy-done.2, bf16[128,6,2048]{2,1,0:T(8,128)(2,1)} %gather.7, pred[128,6]{1,0:T(8,128)(4,1)S(1)} %copy-done.4), kind=kLoop, calls=%fused_computation.1 | loop fusion | flops 6029312 | bytes 4198144 | tf_op jit(solution)/shard_map/reduce_sum | solution.py:77
  287.7 4.4 %fusion.17 = bf16[128,2048]{1,0:T(8,128)(2,1)} fusion(f32[128,2048]{1,0:T(8,128)S(1)} %multiply_reduce_fusion, bf16[128,1408]{0,1:T(8,128)(2,1)S(1)} %bitcast.61, bf16[1408,2048]{1,0:T(8,128)(2,1)} %param.23, bf16[128,2048]{1,0:T(8,128)(2,1)S(1)} %copy-done.1), kind=kOutput, calls=%fused_computation.24 | convolution fusion | flops 739246080 | bytes 8224768 | tf_op jit(solution)/shard_map/dot_general | solution.py:71
  (41 shorter events, 0.8 us)
Async XLA Ops:
  6.5 189.8 %copy-start = (bf16[2048,352]{0,1:T(8,128)(2,1)S(1)}, bf16[2048,352]{0,1:T(8,128)(2,1)}, u32[]{:S(2)}) copy-start(bf16[2048,352]{0,1:T(8,128)(2,1)} %param.21) | copy-start | bytes 4325380
  6.5 2.2 copy-start.1
  6.5 3.0 %copy-start.3 = (f32[2048]{0:T(1024)S(1)}, f32[2048]{0:T(1024)}, u32[]{:S(2)}) copy-start(f32[2048]{0:T(1024)} %param.13) | copy-start | bytes 24580
  6.5 3.2 %copy-start.8 = (s32[128,6]{0,1:T(8,128)S(1)}, s32[128,6]{0,1:T(8,128)}, u32[]{:S(2)}) copy-start(s32[128,6]{0,1:T(8,128)} %param.14) | copy-start | bytes 9220
  6.5 3.2 %copy-start.7 = (s32[128,6]{0,1:T(8,128)S(1)}, s32[128,6]{0,1:T(8,128)}, u32[]{:S(2)}) copy-start(s32[128,6]{0,1:T(8,128)} %param.15) | copy-start | bytes 9220
  6.5 3.2 %copy-start.9 = (s32[128,6]{0,1:T(8,128)S(1)}, s32[128,6]{0,1:T(8,128)}, u32[]{:S(2)}) copy-start(s32[128,6]{0,1:T(8,128)} %param.16) | copy-start | bytes 9220
  6.6 106.1 %all-gather.6.cloned.1.call-start = ((), (), s32[]{:S(2)}) async-start(), calls=%async_computation.4 | async-start | bytes 7208960 | tf_op jit(solution)/shard_map/all_gather | solution.py:51
  7.3 114.4 %all-gather.4.cloned.1.call-start = ((), (), s32[]{:S(2)}) async-start(), calls=%async_computation.3 | async-start | bytes 7208960 | tf_op jit(solution)/shard_map/all_gather | solution.py:50
  8.0 137.0 %all-gather.8.cloned.1.call-start = ((), (), s32[]{:S(2)}) async-start(), calls=%async_computation.5 | async-start | bytes 7208960 | tf_op jit(solution)/shard_map/all_gather | solution.py:52
  9.0 0.6 copy-start.6
  10.4 102.3 %copy-start.5 = (pred[128,6]{0,1:T(8,128)(4,1)}, pred[128,6]{0,1:T(8,128)(4,1)S(1)}, u32[]{:S(2)}) copy-start(pred[128,6]{0,1:T(8,128)(4,1)S(1)} %get-tuple-element.8) | copy-start | bytes 2308
  162.9 99.2 %all-to-all-start.2 = ((bf16[8,2,64,2048]{3,2,1,0:T(8,128)(2,1)}), bf16[8,2,64,2048]{3,2,1,0:T(8,128)(2,1)}, u32[]{:S(2)}, u32[]{:S(2)}) async-start(bf16[8,2,64,2048]{3,2,1,0:T(8,128)(2,1)} %copy.39), calls=%async_computation.2 | async-start | bytes 8388608 | tf_op jit(solution)/shard_map/all_to_all | solution.py:59
  168.4 8.6 %collective-permute-start = (bf16[128,2048]{1,0:T(8,128)(2,1)S(1)}, bf16[128,2048]{1,0:T(8,128)(2,1)S(1)}, u32[]{:S(2)}, u32[]{:S(2)}) collective-permute-start(bf16[128,2048]{1,0:T(8,128)(2,1)S(1)} %fusion.33), channel_id=1, source_target_pairs={{0,1},{1,2},{2,3},{3,0},{4,5},{5,6},{6,7},{7,4},{8,9},{9,10},{10,1... | collective-permute-start | bytes 1572872 | tf_op jit(solution)/shard_map/ppermute | solution.py:63
  177.0 8.6 %collective-permute-start.1 = (bf16[128,2048]{1,0:T(8,128)(2,1)S(1)}, bf16[128,2048]{1,0:T(8,128)(2,1)S(1)}, u32[]{:S(2)}, u32[]{:S(2)}) collective-permute-start(bf16[128,2048]{1,0:T(8,128)(2,1)S(1)} %collective-permute-done), channel_id=1, source_target_pairs={{0,1},{1,2},{2,3},{3,0},{4,5},{5,6},{6,7},{7,4},{8,9},{9,10},{10,1... | collective-permute-start | bytes 1572872 | tf_op jit(solution)/shard_map/ppermute | solution.py:63
  185.6 8.6 %collective-permute-start.2 = (bf16[128,2048]{1,0:T(8,128)(2,1)S(1)}, bf16[128,2048]{1,0:T(8,128)(2,1)S(1)}, u32[]{:S(2)}, u32[]{:S(2)}) collective-permute-start(bf16[128,2048]{1,0:T(8,128)(2,1)S(1)} %collective-permute-done.1), channel_id=1, source_target_pairs={{0,1},{1,2},{2,3},{3,0},{4,5},{5,6},{6,7},{7,4},{8,9},{9,10},{10,1... | collective-permute-start | bytes 1572872 | tf_op jit(solution)/shard_map/ppermute | solution.py:63
  195.3 2.1 copy-start.10
  262.1 25.6 %all-to-all-start = ((bf16[4,128,352]{1,2,0:T(8,128)(2,1)}), bf16[4,128,352]{1,2,0:T(8,128)(2,1)S(1)}, u32[]{:S(2)}, u32[]{:S(2)}) async-start(bf16[4,128,352]{1,2,0:T(8,128)(2,1)} %bitcast.59), calls=%async_computation | async-start | bytes 720896 | tf_op jit(solution)/shard_map/all_to_all | solution.py:70
  275.4 6.3 %copy-start.2 = (f32[128,6]{1,0:T(8,128)S(1)}, f32[128,6]{1,0:T(8,128)}, u32[]{:S(2)}) copy-start(f32[128,6]{1,0:T(8,128)} %copy.41) | copy-start | bytes 9220
  275.4 6.3 %copy-start.4 = (pred[128,6]{1,0:T(8,128)(4,1)S(1)}, pred[128,6]{1,0:T(8,128)(4,1)}, u32[]{:S(2)}) copy-start(pred[128,6]{1,0:T(8,128)(4,1)} %copy.36) | copy-start | bytes 2308
Sparse Core Ops, SparseCore 0:
  8.9 46.0 all-gather.5
  56.6 43.3 all-gather.3
  101.6 43.3 all-gather.7
